TPU v7x, 128 devices: a whole 4x4x4 slice. The times are simulated.
128 devices in a mesh: expert: 4 (over x_lo, core), shard: 32 (over z, y, x_hi).
Axes of the slice: x: 4 (x_hi: 2, x_lo: 2; x = x_hi * 2 + x_lo), y: 4, z: 4, core: 2. Of those that a mesh axis runs over, the one named last changes fastest.
Arguments:
- master_gate: float32 [64, 2048, 1024], P('expert', 'shard'), may hold values from -0.25 to 0.25
- master_up: float32 [64, 2048, 1024], P('expert', 'shard'), may hold values from -0.25 to 0.25
- master_down: float32 [64, 1024, 2048], P('expert', None, 'shard'), may hold values from -0.375 to 0.375
- router_weight: float32 [2048, 64], P('shard', 'expert'), may hold values from -0.125 to 0.125
- router_gain: float32 [2048], P('shard'), may hold values from 0.25 to 1.75
Outputs:
- final_gate: bfloat16 [64, 2048, 1024], P('expert', None, 'shard')
- final_up: bfloat16 [64, 2048, 1024], P('expert', None, 'shard')
- final_down: bfloat16 [64, 1024, 2048], P('expert', 'shard')
- scale_gate: float32 [64, 1024], P('expert', 'shard')
- scale_up: float32 [64, 1024], P('expert', 'shard')
- scale_down: float32 [64, 1024], P('expert', 'shard')
- serve_router: bfloat16 [2048, 64], replicated
All inputs are finite; a program needn't handle non-finite values.
Results may differ from a plain program's by a relative error of at most 0.001.
Values may be sent and summed in bfloat16 or wider, within the bound.
A program may use at most 128 MiB of HBM per device.

v0:
```python
import jax
import jax.numpy as jnp
from jax import lax
from jax.sharding import Mesh
from jax.sharding import PartitionSpec as P

SHARD = ("shard_0", "shard_1", "shard_2")
EXPERT = ("expert_0", "expert_1")


def total_of_pieces(value, axis):
    return lax.all_gather(value, axis).sum(0)


def in_order(pieces, dim):
    pieces = jnp.moveaxis(pieces, 0, dim)
    lengths = pieces.shape
    return pieces.reshape(*lengths[:dim], lengths[dim] * lengths[dim + 1], *lengths[dim + 2 :])


def gather_in_order(value, axes, order):
    pieces = value[None]
    for k in order:
        pieces = lax.all_gather(pieces, axes[k], axis=0, tiled=True)
    current = [lax.axis_size(axes[k]) for k in reversed(order)]
    pieces = pieces.reshape(*current, *value.shape)
    turned = sorted(range(len(order)), key=lambda place: order[len(order) - 1 - place])
    return pieces.transpose(*turned, *range(len(order), pieces.ndim)).reshape(-1, *value.shape)


def whole_of(value, axes, order, dim):
    return in_order(gather_in_order(value, axes, order), dim)


def on_device(master_gate, master_up, master_down, router_weight, router_gain):
    total_gate, total_up, total_down = (
        total_of_pieces(jnp.sum(master_gate * master_gate, axis=1), SHARD),
        total_of_pieces(jnp.sum(master_up * master_up, axis=1), SHARD),
        total_of_pieces(jnp.sum(master_down * master_down, axis=2), SHARD),
    )
    scale_gate = jnp.sqrt(total_gate)
    scale_up = jnp.sqrt(total_up)
    scale_down = jnp.sqrt(total_down)
    narrow_gate, narrow_up, narrow_down = (
        (master_gate / jnp.expand_dims(scale_gate, 1)).astype(jnp.bfloat16),
        (master_up / jnp.expand_dims(scale_up, 1)).astype(jnp.bfloat16),
        (master_down / jnp.expand_dims(scale_down, 2)).astype(jnp.bfloat16),
    )
    final_gate, final_up = (
        lax.all_to_all(narrow_gate, SHARD, split_axis=2, concat_axis=1, tiled=True),
        lax.all_to_all(narrow_up, SHARD, split_axis=2, concat_axis=1, tiled=True),
    )
    final_down = lax.all_to_all(narrow_down, SHARD, split_axis=1, concat_axis=2, tiled=True)
    scale_gate = lax.dynamic_slice_in_dim(
        scale_gate, lax.axis_index(SHARD) * final_gate.shape[2], final_gate.shape[2], axis=1
    )
    scale_up = lax.dynamic_slice_in_dim(
        scale_up, lax.axis_index(SHARD) * final_up.shape[2], final_up.shape[2], axis=1
    )
    scale_down = lax.dynamic_slice_in_dim(
        scale_down, lax.axis_index(SHARD) * final_down.shape[1], final_down.shape[1], axis=1
    )
    part_router = (router_weight * router_gain[:, None]).astype(jnp.bfloat16)
    row_router = whole_of(part_router, SHARD, (2, 0, 1), 0)
    serve_router = whole_of(row_router, EXPERT, (0, 1), 1)
    return (final_gate, final_up, final_down, scale_gate, scale_up, scale_down, serve_router)


def solution(mesh):
    torus = Mesh(
        mesh.devices.reshape(2, 2, 4, 4, 2),
        ("expert_0", "expert_1", "shard_0", "shard_1", "shard_2"),
    )
    return jax.shard_map(
        on_device,
        mesh=torus,
        in_specs=(
            P(EXPERT, SHARD, None),
            P(EXPERT, SHARD, None),
            P(EXPERT, None, SHARD),
            P(SHARD, EXPERT),
            P(SHARD),
        ),
        out_specs=(
            P(EXPERT, None, SHARD),
            P(EXPERT, None, SHARD),
            P(EXPERT, SHARD, None),
            P(EXPERT, SHARD),
            P(EXPERT, SHARD),
            P(EXPERT, SHARD),
            P(),
        ),
        check_vma=False,
    )
```

profile of v0, /device:TPU:1, one launch (start us, length us, event | category | flops | bytes accessed | tf_op | source)
XLA Modules:
  0.0 398.6 jit_solution(14546526943388077372)
XLA Ops:
  7.2 3.4 multiply_reduce_fusion.2
  10.7 3.4 multiply_reduce_fusion.1
  14.2 3.4 multiply_reduce_fusion
  17.6 8.1 %copy.42 = f32[16,64,1024]{1,0,2:T(8,128)} copy(f32[16,64,1024]{2,1,0:T(8,128)} %param.5) | data formatting | bytes 8388608 | tf_op args[0]
  25.8 57.4 %all-gather.9.cloned.1.call-done = f32[512,1024]{1,0:T(8,128)} async-done(((f32[16,1024]{1,0:T(8,128)}), f32[512,1024]{1,0:T(8,128)}) %all-gather.9.cloned.1.call-update) | async-done | bytes 2097168 | tf_op jit(solution)/shard_map/all_gather | solution.py:12
  85.1 6.9 %fusion.1 = bf16[1024,16,64]{2,1,0:T(8,128)(2,1)} fusion(f32[16,64,1024]{1,0,2:T(8,128)} %copy.42, f32[16,1024]{0,1:T(8,128)S(1)} %copy.41), kind=kLoop, calls=%fused_computation.12 | loop fusion | flops 2097152 | bytes 6356992
  91.9 7.9 %reshape.47 = bf16[32,2,16384]{2,1,0:T(2,128)(2,1)} reshape(bf16[1024,16,64]{2,1,0:T(8,128)(2,1)} %fusion.1) | data formatting | bytes 4194304
  99.8 5.9 %all-to-all-start = ((bf16[32,2,16384]{2,1,0:T(2,128)(2,1)}), bf16[32,2,16384]{2,1,0:T(2,128)(2,1)S(1)}, u32[]{:S(2)}, u32[]{:S(2)}) async-start(bf16[32,2,16384]{2,1,0:T(2,128)(2,1)} %reshape.47), calls=%async_computation | async-start | bytes 4194304 | tf_op jit(solution)/shard_map/all_to_all | solution.py:50
  105.7 8.1 %copy.46 = f32[16,64,1024]{1,0,2:T(8,128)} copy(f32[16,64,1024]{2,1,0:T(8,128)} %param.6) | data formatting | bytes 8388608 | tf_op args[1]
  113.8 51.8 %all-gather.11.cloned.1.call-done = f32[512,1024]{1,0:T(8,128)} async-done(((f32[16,1024]{1,0:T(8,128)}), f32[512,1024]{1,0:T(8,128)}) %all-gather.11.cloned.1.call-update) | async-done | bytes 2097168 | tf_op jit(solution)/shard_map/all_gather | solution.py:12
  167.5 6.9 %fusion.2 = bf16[1024,16,64]{2,1,0:T(8,128)(2,1)} fusion(f32[16,64,1024]{1,0,2:T(8,128)} %copy.46, f32[16,1024]{0,1:T(8,128)S(1)} %copy.45), kind=kLoop, calls=%fused_computation.13 | loop fusion | flops 2097152 | bytes 6356992
  174.4 7.9 %reshape.49 = bf16[32,2,16384]{2,1,0:T(2,128)(2,1)} reshape(bf16[1024,16,64]{2,1,0:T(8,128)(2,1)} %fusion.2) | data formatting | bytes 4194304
  182.2 6.0 %all-to-all-start.1 = ((bf16[32,2,16384]{2,1,0:T(2,128)(2,1)}), bf16[32,2,16384]{2,1,0:T(2,128)(2,1)}, u32[]{:S(2)}, u32[]{:S(2)}) async-start(bf16[32,2,16384]{2,1,0:T(2,128)(2,1)} %reshape.49), calls=%async_computation.1 | async-start | bytes 4194304 | tf_op jit(solution)/shard_map/all_to_all | solution.py:51
  188.3 8.1 %copy.50 = f32[16,1024,64]{2,0,1:T(8,128)} copy(f32[16,1024,64]{1,2,0:T(8,128)} %param.7) | data formatting | bytes 8388608 | tf_op args[2]
  196.4 51.6 %all-gather.13.cloned.1.call-done = f32[512,1024]{1,0:T(8,128)} async-done(((f32[16,1024]{1,0:T(8,128)}), f32[512,1024]{1,0:T(8,128)}) %all-gather.13.cloned.1.call-update) | async-done | bytes 2097168 | tf_op jit(solution)/shard_map/all_gather | solution.py:12
  250.0 6.9 %fusion.3 = bf16[1024,16,64]{2,1,0:T(8,128)(2,1)} fusion(f32[16,1024,64]{2,0,1:T(8,128)} %copy.50, f32[16,1024]{0,1:T(8,128)S(1)} %copy.49), kind=kLoop, calls=%fused_computation.14 | loop fusion | flops 2097152 | bytes 6356992
  256.8 7.9 %reshape.51 = bf16[32,2,16384]{2,1,0:T(2,128)(2,1)} reshape(bf16[1024,16,64]{2,1,0:T(8,128)(2,1)} %fusion.3) | data formatting | bytes 4194304
  264.7 6.0 %all-to-all-start.2 = ((bf16[32,2,16384]{2,1,0:T(2,128)(2,1)}), bf16[32,2,16384]{2,1,0:T(2,128)(2,1)}, u32[]{:S(2)}, u32[]{:S(2)}) async-start(bf16[32,2,16384]{2,1,0:T(2,128)(2,1)} %reshape.51), calls=%async_computation.2 | async-start | bytes 4194304 | tf_op jit(solution)/shard_map/all_to_all | solution.py:53
  270.8 23.2 %all-gather.4 = bf16[2,64,16]{1,2,0:T(8,128)(2,1)S(1)} all-gather(bf16[1,64,16]{1,2,0:T(8,128)(2,1)S(1)} %fusion), channel_id=5, replica_groups=mesh['expert_0'=2,'expert_1'=2,'shard_0'=4,'shard_1'=4,'shard_2'=2] {'sh..., dimensions={0}, use_global_device_ids=true | all-gather | bytes 6144 | tf_op jit(solution)/shard_map/all_gather | solution.py:24
  294.0 10.0 %all_gather.40 = bf16[8,64,16]{1,2,0:T(8,128)(2,1)S(1)} all-gather(bf16[2,64,16]{1,2,0:T(8,128)(2,1)S(1)} %all-gather.4), channel_id=1, replica_groups=mesh['expert_0'=2,'expert_1'=2,'shard_0'=4,'shard_1'=4,'shard_2'=2] {'sh..., dimensions={0}, use_global_device_ids=true | all-gather | bytes 20480 | tf_op jit(solution)/shard_map/all_gather | solution.py:24
  304.0 9.3 %all_gather.41 = bf16[32,64,16]{1,2,0:T(8,128)(2,1)S(1)} all-gather(bf16[8,64,16]{1,2,0:T(8,128)(2,1)S(1)} %all_gather.40), channel_id=1, replica_groups=mesh['expert_0'=2,'expert_1'=2,'shard_0'=4,'shard_1'=4,'shard_2'=2] {'sh..., dimensions={0}, use_global_device_ids=true | all-gather | bytes 81920 | tf_op jit(solution)/shard_map/all_gather | solution.py:24
  313.6 3.8 all_gather.42
  317.4 11.9 %all_gather.43 = bf16[4,2048,16]{1,2,0:T(8,128)(2,1)S(1)} all-gather(bf16[2,2048,16]{1,2,0:T(8,128)(2,1)S(1)} %all_gather.42), channel_id=1, replica_groups=mesh['expert_0'=2,'expert_1'=2,'shard_0'=4,'shard_1'=4,'shard_2'=2] {'ex..., dimensions={0}, use_global_device_ids=true | all-gather | bytes 393216 | tf_op jit(solution)/shard_map/all_gather | solution.py:24
  331.4 4.0 %reshape.48 = bf16[1024,16,64]{2,1,0:T(8,128)(2,1)} reshape(bf16[32,2,16384]{2,1,0:T(2,128)(2,1)S(1)} %all-to-all-done) | data formatting | bytes 4194304
  335.4 6.9 %copy.44 = bf16[16,32,64,32]{2,1,3,0:T(8,128)(2,1)} copy(bf16[16,32,64,32]{2,0,3,1:T(8,128)(2,1)} %bitcast.47) | data formatting | bytes 4194304 | tf_op jit(solution)/shard_map/all_to_all | solution.py:50
  342.2 6.7 %all_to_all.42 = bf16[16,2048,32]{1,2,0:T(8,128)(2,1)} reshape(bf16[16,32,64,32]{2,1,3,0:T(8,128)(2,1)} %copy.44) | data formatting | bytes 4194304 | tf_op jit(solution)/shard_map/all_to_all | solution.py:50
  349.0 7.9 %reshape.50 = bf16[1024,16,64]{2,1,0:T(8,128)(2,1)} reshape(bf16[32,2,16384]{2,1,0:T(2,128)(2,1)} %all-to-all-done.1) | data formatting | bytes 4194304
  356.9 6.9 %copy.48 = bf16[16,32,64,32]{2,1,3,0:T(8,128)(2,1)} copy(bf16[16,32,64,32]{2,0,3,1:T(8,128)(2,1)} %bitcast.48) | data formatting | bytes 4194304 | tf_op jit(solution)/shard_map/all_to_all | solution.py:51
  363.8 6.7 %all_to_all.46 = bf16[16,2048,32]{1,2,0:T(8,128)(2,1)} reshape(bf16[16,32,64,32]{2,1,3,0:T(8,128)(2,1)} %copy.48) | data formatting | bytes 4194304 | tf_op jit(solution)/shard_map/all_to_all | solution.py:51
  370.5 7.9 %reshape.52 = bf16[1024,16,64]{2,1,0:T(8,128)(2,1)} reshape(bf16[32,2,16384]{2,1,0:T(2,128)(2,1)} %all-to-all-done.2) | data formatting | bytes 4194304
  378.5 6.9 %copy.52 = bf16[16,32,32,64]{3,2,1,0:T(8,128)(2,1)} copy(bf16[16,32,32,64]{3,0,1,2:T(8,128)(2,1)} %bitcast.49) | data formatting | bytes 4194304 | tf_op jit(solution)/shard_map/all_to_all | solution.py:53
  385.3 6.7 %all_to_all.50 = bf16[16,32,2048]{2,1,0:T(8,128)(2,1)} reshape(bf16[16,32,32,64]{3,2,1,0:T(8,128)(2,1)} %copy.52) | data formatting | bytes 4194304 | tf_op jit(solution)/shard_map/all_to_all | solution.py:53
  (28 shorter events, 8.3 us)
Async XLA Ops:
  7.2 76.0 %all-gather.9.cloned.1.call-start = ((), (), s32[]{:S(2)}) async-start(), calls=%async_computation.3 | async-start | bytes 2162688 | tf_op jit(solution)/shard_map/all_gather | solution.py:12
  10.7 154.9 %all-gather.11.cloned.1.call-start = ((), (), s32[]{:S(2)}) async-start(), calls=%async_computation.4 | async-start | bytes 2162688 | tf_op jit(solution)/shard_map/all_gather | solution.py:12
  14.1 233.9 %all-gather.13.cloned.1.call-start = ((), (), s32[]{:S(2)}) async-start(), calls=%async_computation.5 | async-start | bytes 2162688 | tf_op jit(solution)/shard_map/all_gather | solution.py:12
  99.8 82.4 %all-to-all-start = ((bf16[32,2,16384]{2,1,0:T(2,128)(2,1)}), bf16[32,2,16384]{2,1,0:T(2,128)(2,1)S(1)}, u32[]{:S(2)}, u32[]{:S(2)}) async-start(bf16[32,2,16384]{2,1,0:T(2,128)(2,1)} %reshape.47), calls=%async_computation | async-start | bytes 4194304 | tf_op jit(solution)/shard_map/all_to_all | solution.py:50
  182.2 82.5 %all-to-all-start.1 = ((bf16[32,2,16384]{2,1,0:T(2,128)(2,1)}), bf16[32,2,16384]{2,1,0:T(2,128)(2,1)}, u32[]{:S(2)}, u32[]{:S(2)}) async-start(bf16[32,2,16384]{2,1,0:T(2,128)(2,1)} %reshape.49), calls=%async_computation.1 | async-start | bytes 4194304 | tf_op jit(solution)/shard_map/all_to_all | solution.py:51
  256.8 14.0 %copy-start = (f32[64,16]{0,1:T(8,128)S(1)}, f32[64,16]{0,1:T(8,128)}, u32[]{:S(2)}) copy-start(f32[64,16]{0,1:T(8,128)} %param.8) | copy-start | bytes 12292
  256.8 14.0 %copy-start.1 = (f32[64]{0:T(128)S(1)}, f32[64]{0:T(128)}, u32[]{:S(2)}) copy-start(f32[64]{0:T(128)} %param.9) | copy-start | bytes 772
  264.7 105.8 %all-to-all-start.2 = ((bf16[32,2,16384]{2,1,0:T(2,128)(2,1)}), bf16[32,2,16384]{2,1,0:T(2,128)(2,1)}, u32[]{:S(2)}, u32[]{:S(2)}) async-start(bf16[32,2,16384]{2,1,0:T(2,128)(2,1)} %reshape.51), calls=%async_computation.2 | async-start | bytes 4194304 | tf_op jit(solution)/shard_map/all_to_all | solution.py:53
Sparse Core Ops, SparseCore 0:
  11.6 71.4 all-gather.8
  86.8 78.7 all-gather.10
  169.2 78.7 all-gather.12
where the time goes:
time: 401 us; the launch traced here: 399 us
  waiting for transfers between devices  161 us (40%)
  local copies, waits for them, and re-layouts  112 us (28%)
  blocking collectives  58.2 us (15%)
  other arithmetic  36 us (9%)
  starting transfers between devices  18.1 us (5%)
  between operations  13.9 us (3%)
    all_gather x3, waiting for transfers between devices, total_of_pieces(): return lax.all_gather(value, axis).sum(0)  161 us
    unnamed x13, local copies, waits for them, and re-layouts  67.8 us
    all_gather x5, blocking collectives, gather_in_order(): pieces = lax.all_gather(pieces, axes[k], axis=0, tiled=True)  58.2 us
    unnamed x4, other arithmetic  20.6 us
    all_to_all x2, local copies, waits for them, and re-layouts, on_device(): lax.all_to_all(narrow_down, SHARD, split_axis=1, concat_axis=2, tiled=True)  13.6 us
    all_to_all x2, local copies, waits for them, and re-layouts, on_device(): lax.all_to_all(narrow_gate, SHARD, split_axis=2, concat_axis=1, tiled=True)  13.6 us
    all_to_all x2, local copies, waits for them, and re-layouts, on_device(): lax.all_to_all(narrow_up, SHARD, split_axis=2, concat_axis=1, tiled=True)  13.6 us
  transfers between devices with their start and end apart: 6, of which 3 were waited for; matrix products, arithmetic and copies ran while one was open for 27% of the time, Pallas kernels for 0%

commit v1 on v0

--- a/solution.py
+++ b/solution.py
@@ -21,7 +21,9 @@
 def gather_in_order(value, axes, order):
     pieces = value[None]
     for k in order:
-        pieces = lax.all_gather(pieces, axes[k], axis=0, tiled=True)
+        pieces = jnp.concatenate(
+            lax.all_to_all(jnp.stack([pieces] * lax.axis_size(axes[k])), axes[k], 0, 0), axis=0
+        )
     current = [lax.axis_size(axes[k]) for k in reversed(order)]
     pieces = pieces.reshape(*current, *value.shape)
     turned = sorted(range(len(order)), key=lambda place: order[len(order) - 1 - place])

time: 401 us -> 346 us (0.86)
  waiting for transfers between devices: 161 us -> 121 us
  blocking collectives: 58.2 us -> 26.3 us
  starting transfers between devices: 18.1 us -> 30.1 us
    all_gather x5 -> x0, blocking collectives: 58.2 us -> none  [gather_in_order(): pieces = lax.all_gather(pieces, axes[k], axis=0, tiled=True)]
    all_gather x3, waiting for transfers between devices: 161 us -> 121 us  [total_of_pieces(): return lax.all_gather(value, axis).sum(0)]
    all_to_all x0 -> x3, blocking collectives: none -> 26.3 us  [gather_in_order(): lax.all_to_all(jnp.stack([pieces] * lax.axis_size(axes[k])), axes[k], 0, 0)]
    all_to_all x0 -> x2, starting transfers between devices: none -> 11.8 us  [gather_in_order(): lax.all_to_all(jnp.stack([pieces] * lax.axis_size(axes[k])), axes[k], 0, 0)]
    unnamed x13 -> x21, local copies, waits for them, and re-layouts: 67.8 us -> 68.5 us
  transfers between devices with their start and end apart: 6 -> 8, of which waited for: 3 -> 3; matrix products, arithmetic and copies ran while one was open for 27% -> 33% of each run, Pallas kernels for 0% -> 0%
where the time goes in v1:
time: 346 us; the launch traced here: 341 us
  waiting for transfers between devices  121 us (35%)
  local copies, waits for them, and re-layouts  112 us (32%)
  other arithmetic  37.3 us (11%)
  starting transfers between devices  30.1 us (9%)
  blocking collectives  26.3 us (8%)
  between operations  13.9 us (4%)
    all_gather x3, waiting for transfers between devices, total_of_pieces(): return lax.all_gather(value, axis).sum(0)  121 us
    unnamed x21, local copies, waits for them, and re-layouts  68.5 us
    all_to_all x3, blocking collectives, gather_in_order(): lax.all_to_all(jnp.stack([pieces] * lax.axis_size(axes[k])), axes[k], 0, 0)  26.3 us
    unnamed x4, other arithmetic  20.6 us
    all_to_all x2, local copies, waits for them, and re-layouts, on_device(): lax.all_to_all(narrow_gate, SHARD, split_axis=2, concat_axis=1, tiled=True)  13.6 us
    all_to_all x2, local copies, waits for them, and re-layouts, on_device(): lax.all_to_all(narrow_up, SHARD, split_axis=2, concat_axis=1, tiled=True)  13.6 us
    all_to_all x2, local copies, waits for them, and re-layouts, on_device(): lax.all_to_all(narrow_down, SHARD, split_axis=1, concat_axis=2, tiled=True)  13.6 us
    all_to_all x2, starting transfers between devices, gather_in_order(): lax.all_to_all(jnp.stack([pieces] * lax.axis_size(axes[k])), axes[k], 0, 0)  11.8 us
  transfers between devices with their start and end apart: 8, of which 3 were waited for; matrix products, arithmetic and copies ran while one was open for 33% of the time, Pallas kernels for 0%

profile of v1, /device:TPU:1, one launch (start us, length us, event | category | flops | bytes accessed | tf_op | source)
XLA Modules:
  0.0 340.7 jit_solution(9779688366531599395)
XLA Ops:
  7.2 3.4 %multiply_reduce_fusion.2 = f32[16,1024]{1,0:T(8,128)} fusion(f32[16,64,1024]{2,1,0:T(8,128)} %param.5), kind=kLoop, calls=%fused_computation.5 | loop fusion | flops 2080768 | bytes 4259840 | tf_op jit(solution)/shard_map/reduce_sum | solution.py:39
  10.7 3.4 %multiply_reduce_fusion.1 = f32[16,1024]{1,0:T(8,128)} fusion(f32[16,64,1024]{2,1,0:T(8,128)} %param.6), kind=kLoop, calls=%fused_computation.4 | loop fusion | flops 2080768 | bytes 4259840 | tf_op jit(solution)/shard_map/reduce_sum | solution.py:40
  14.3 8.8 %all_to_all.79 = bf16[2,2,512]{2,1,0:T(2,128)(2,1)S(1)} all-to-all(bf16[2,2,512]{2,1,0:T(2,128)(2,1)S(1)} %reshape.45), channel_id=1, replica_groups=mesh['expert_0'=2,'expert_1'=2,'shard_0'=4,'shard_1'=4,'shard_2'=2] {'sh..., dimensions={0} | all-to-all | bytes 8192 | tf_op jit(solution)/shard_map/all_to_all | solution.py:25
  23.3 9.0 %all_to_all.80 = bf16[4,2,1024]{2,1,0:T(2,128)(2,1)S(1)} all-to-all(bf16[4,2,1024]{2,1,0:T(2,128)(2,1)S(1)} %reshape.47), channel_id=1, replica_groups=mesh['expert_0'=2,'expert_1'=2,'shard_0'=4,'shard_1'=4,'shard_2'=2] {'sh..., dimensions={0} | all-to-all | bytes 32768 | tf_op jit(solution)/shard_map/all_to_all | solution.py:25
  32.6 8.5 %all_to_all.81 = bf16[4,2,4096]{2,1,0:T(2,128)(2,1)S(1)} all-to-all(bf16[4,2,4096]{2,1,0:T(2,128)(2,1)S(1)} %reshape.49), channel_id=1, replica_groups=mesh['expert_0'=2,'expert_1'=2,'shard_0'=4,'shard_1'=4,'shard_2'=2] {'sh..., dimensions={0} | all-to-all | bytes 131072 | tf_op jit(solution)/shard_map/all_to_all | solution.py:25
  42.2 3.4 all-to-all-start.6
  45.6 3.4 %multiply_reduce_fusion = f32[16,1024]{1,0:T(8,128)} fusion(f32[16,1024,64]{1,2,0:T(8,128)} %param.7), kind=kLoop, calls=%fused_computation.3 | loop fusion | flops 2080768 | bytes 4259840 | tf_op jit(solution)/shard_map/reduce_sum | solution.py:41
  49.0 8.1 %copy.49 = f32[16,64,1024]{1,0,2:T(8,128)} copy(f32[16,64,1024]{2,1,0:T(8,128)} %param.5) | data formatting | bytes 8388608 | tf_op args[0]
  57.9 8.5 %all-to-all-start.7 = ((bf16[2,2,2048,16]{2,3,1,0:T(8,128)(2,1)}), bf16[2,2,2048,16]{2,3,1,0:T(8,128)(2,1)S(1)}, u32[]{:S(2)}, u32[]{:S(2)}) async-start(bf16[2,2,2048,16]{2,3,1,0:T(8,128)(2,1)} %pad_maximum_fusion), calls=%async_computation.7 | async-start | bytes 524288 | tf_op jit(solution)/shard_map/all_to_all | solution.py:25
  66.4 16.8 %all-gather.7.cloned.1.call-done = f32[512,1024]{1,0:T(8,128)} async-done(((f32[16,1024]{1,0:T(8,128)}), f32[512,1024]{1,0:T(8,128)}) %all-gather.7.cloned.1.call-update) | async-done | bytes 2097168 | tf_op jit(solution)/shard_map/all_gather | solution.py:12
  85.1 6.9 %fusion.1 = bf16[1024,16,64]{2,1,0:T(8,128)(2,1)} fusion(f32[16,64,1024]{1,0,2:T(8,128)} %copy.49, f32[16,1024]{0,1:T(8,128)S(1)} %copy.48), kind=kLoop, calls=%fused_computation.14 | loop fusion | flops 2097152 | bytes 6356992
  91.9 7.9 %reshape.39 = bf16[32,2,16384]{2,1,0:T(2,128)(2,1)} reshape(bf16[1024,16,64]{2,1,0:T(8,128)(2,1)} %fusion.1) | data formatting | bytes 4194304
  99.8 5.9 %all-to-all-start = ((bf16[32,2,16384]{2,1,0:T(2,128)(2,1)}), bf16[32,2,16384]{2,1,0:T(2,128)(2,1)S(1)}, u32[]{:S(2)}, u32[]{:S(2)}) async-start(bf16[32,2,16384]{2,1,0:T(2,128)(2,1)} %reshape.39), calls=%async_computation | async-start | bytes 4194304 | tf_op jit(solution)/shard_map/all_to_all | solution.py:52
  105.7 8.1 %copy.53 = f32[16,64,1024]{1,0,2:T(8,128)} copy(f32[16,64,1024]{2,1,0:T(8,128)} %param.6) | data formatting | bytes 8388608 | tf_op args[1]
  113.8 51.8 %all-gather.9.cloned.1.call-done = f32[512,1024]{1,0:T(8,128)} async-done(((f32[16,1024]{1,0:T(8,128)}), f32[512,1024]{1,0:T(8,128)}) %all-gather.9.cloned.1.call-update) | async-done | bytes 2097168 | tf_op jit(solution)/shard_map/all_gather | solution.py:12
  167.5 6.9 %fusion.2 = bf16[1024,16,64]{2,1,0:T(8,128)(2,1)} fusion(f32[16,64,1024]{1,0,2:T(8,128)} %copy.53, f32[16,1024]{0,1:T(8,128)S(1)} %copy.52), kind=kLoop, calls=%fused_computation.15 | loop fusion | flops 2097152 | bytes 6356992
  174.4 7.9 %reshape.41 = bf16[32,2,16384]{2,1,0:T(2,128)(2,1)} reshape(bf16[1024,16,64]{2,1,0:T(8,128)(2,1)} %fusion.2) | data formatting | bytes 4194304
  182.3 6.2 %all-to-all-start.1 = ((bf16[32,2,16384]{2,1,0:T(2,128)(2,1)}), bf16[32,2,16384]{2,1,0:T(2,128)(2,1)}, u32[]{:S(2)}, u32[]{:S(2)}) async-start(bf16[32,2,16384]{2,1,0:T(2,128)(2,1)} %reshape.41), calls=%async_computation.1 | async-start | bytes 4194304 | tf_op jit(solution)/shard_map/all_to_all | solution.py:53
  188.5 8.1 %copy.57 = f32[16,1024,64]{2,0,1:T(8,128)} copy(f32[16,1024,64]{1,2,0:T(8,128)} %param.7) | data formatting | bytes 8388608 | tf_op args[2]
  196.6 52.2 %all-gather.11.cloned.1.call-done = f32[512,1024]{1,0:T(8,128)} async-done(((f32[16,1024]{1,0:T(8,128)}), f32[512,1024]{1,0:T(8,128)}) %all-gather.11.cloned.1.call-update) | async-done | bytes 2097168 | tf_op jit(solution)/shard_map/all_gather | solution.py:12
  250.7 6.9 %fusion.3 = bf16[1024,16,64]{2,1,0:T(8,128)(2,1)} fusion(f32[16,1024,64]{2,0,1:T(8,128)} %copy.57, f32[16,1024]{0,1:T(8,128)S(1)} %copy.56), kind=kLoop, calls=%fused_computation.16 | loop fusion | flops 2097152 | bytes 6356992
  257.5 7.9 %reshape.43 = bf16[32,2,16384]{2,1,0:T(2,128)(2,1)} reshape(bf16[1024,16,64]{2,1,0:T(8,128)(2,1)} %fusion.3) | data formatting | bytes 4194304
  265.4 6.0 %all-to-all-start.2 = ((bf16[32,2,16384]{2,1,0:T(2,128)(2,1)}), bf16[32,2,16384]{2,1,0:T(2,128)(2,1)}, u32[]{:S(2)}, u32[]{:S(2)}) async-start(bf16[32,2,16384]{2,1,0:T(2,128)(2,1)} %reshape.43), calls=%async_computation.2 | async-start | bytes 4194304 | tf_op jit(solution)/shard_map/all_to_all | solution.py:55
  273.5 4.0 %reshape.40 = bf16[1024,16,64]{2,1,0:T(8,128)(2,1)} reshape(bf16[32,2,16384]{2,1,0:T(2,128)(2,1)S(1)} %all-to-all-done) | data formatting | bytes 4194304
  277.5 6.9 %copy.51 = bf16[16,32,64,32]{2,1,3,0:T(8,128)(2,1)} copy(bf16[16,32,64,32]{2,0,3,1:T(8,128)(2,1)} %bitcast.58) | data formatting | bytes 4194304 | tf_op jit(solution)/shard_map/all_to_all | solution.py:52
  284.3 6.7 %all_to_all.57 = bf16[16,2048,32]{1,2,0:T(8,128)(2,1)} reshape(bf16[16,32,64,32]{2,1,3,0:T(8,128)(2,1)} %copy.51) | data formatting | bytes 4194304 | tf_op jit(solution)/shard_map/all_to_all | solution.py:52
  291.1 7.9 %reshape.42 = bf16[1024,16,64]{2,1,0:T(8,128)(2,1)} reshape(bf16[32,2,16384]{2,1,0:T(2,128)(2,1)} %all-to-all-done.1) | data formatting | bytes 4194304
  299.0 6.9 %copy.55 = bf16[16,32,64,32]{2,1,3,0:T(8,128)(2,1)} copy(bf16[16,32,64,32]{2,0,3,1:T(8,128)(2,1)} %bitcast.59) | data formatting | bytes 4194304 | tf_op jit(solution)/shard_map/all_to_all | solution.py:53
  305.9 6.7 %all_to_all.61 = bf16[16,2048,32]{1,2,0:T(8,128)(2,1)} reshape(bf16[16,32,64,32]{2,1,3,0:T(8,128)(2,1)} %copy.55) | data formatting | bytes 4194304 | tf_op jit(solution)/shard_map/all_to_all | solution.py:53
  312.6 7.9 %reshape.44 = bf16[1024,16,64]{2,1,0:T(8,128)(2,1)} reshape(bf16[32,2,16384]{2,1,0:T(2,128)(2,1)} %all-to-all-done.2) | data formatting | bytes 4194304
  320.6 6.9 %copy.59 = bf16[16,32,32,64]{3,2,1,0:T(8,128)(2,1)} copy(bf16[16,32,32,64]{3,0,1,2:T(8,128)(2,1)} %bitcast.60) | data formatting | bytes 4194304 | tf_op jit(solution)/shard_map/all_to_all | solution.py:55
  327.4 6.7 %all_to_all.65 = bf16[16,32,2048]{2,1,0:T(8,128)(2,1)} reshape(bf16[16,32,32,64]{3,2,1,0:T(8,128)(2,1)} %copy.59) | data formatting | bytes 4194304 | tf_op jit(solution)/shard_map/all_to_all | solution.py:55
  (42 shorter events, 10.4 us)
Async XLA Ops:
  7.2 7.0 %copy-start = (f32[64,16]{0,1:T(8,128)S(1)}, f32[64,16]{0,1:T(8,128)}, u32[]{:S(2)}) copy-start(f32[64,16]{0,1:T(8,128)} %param.8) | copy-start | bytes 12292
  7.2 7.0 %copy-start.1 = (f32[64]{0:T(128)S(1)}, f32[64]{0:T(128)}, u32[]{:S(2)}) copy-start(f32[64]{0:T(128)} %param.9) | copy-start | bytes 772
  7.2 76.0 %all-gather.7.cloned.1.call-start = ((), (), s32[]{:S(2)}) async-start(), calls=%async_computation.8 | async-start | bytes 2162688 | tf_op jit(solution)/shard_map/all_gather | solution.py:12
  10.7 154.9 %all-gather.9.cloned.1.call-start = ((), (), s32[]{:S(2)}) async-start(), calls=%async_computation.9 | async-start | bytes 2162688 | tf_op jit(solution)/shard_map/all_gather | solution.py:12
  42.2 15.0 %all-to-all-start.6 = ((bf16[2,1,2048,16]{2,3,1,0:T(8,128)(2,1)}), bf16[2,1,2048,16]{2,3,1,0:T(8,128)(2,1)S(1)}, u32[]{:S(2)}, u32[]{:S(2)}) async-start(bf16[2,1,2048,16]{2,3,1,0:T(8,128)(2,1)} %pad_maximum_fusion.1), calls=%async_computation.6 | async-start | bytes 262144 | tf_op jit(solution)/shard_map/all_to_all | solution.py:25
  45.5 203.2 %all-gather.11.cloned.1.call-start = ((), (), s32[]{:S(2)}) async-start(), calls=%async_computation.10 | async-start | bytes 2162688 | tf_op jit(solution)/shard_map/all_gather | solution.py:12
  57.9 41.9 %all-to-all-start.7 = ((bf16[2,2,2048,16]{2,3,1,0:T(8,128)(2,1)}), bf16[2,2,2048,16]{2,3,1,0:T(8,128)(2,1)S(1)}, u32[]{:S(2)}, u32[]{:S(2)}) async-start(bf16[2,2,2048,16]{2,3,1,0:T(8,128)(2,1)} %pad_maximum_fusion), calls=%async_computation.7 | async-start | bytes 524288 | tf_op jit(solution)/shard_map/all_to_all | solution.py:25
  99.8 82.4 %all-to-all-start = ((bf16[32,2,16384]{2,1,0:T(2,128)(2,1)}), bf16[32,2,16384]{2,1,0:T(2,128)(2,1)S(1)}, u32[]{:S(2)}, u32[]{:S(2)}) async-start(bf16[32,2,16384]{2,1,0:T(2,128)(2,1)} %reshape.39), calls=%async_computation | async-start | bytes 4194304 | tf_op jit(solution)/shard_map/all_to_all | solution.py:52
  182.3 83.1 %all-to-all-start.1 = ((bf16[32,2,16384]{2,1,0:T(2,128)(2,1)}), bf16[32,2,16384]{2,1,0:T(2,128)(2,1)}, u32[]{:S(2)}, u32[]{:S(2)}) async-start(bf16[32,2,16384]{2,1,0:T(2,128)(2,1)} %reshape.41), calls=%async_computation.1 | async-start | bytes 4194304 | tf_op jit(solution)/shard_map/all_to_all | solution.py:53
  265.4 47.2 %all-to-all-start.2 = ((bf16[32,2,16384]{2,1,0:T(2,128)(2,1)}), bf16[32,2,16384]{2,1,0:T(2,128)(2,1)}, u32[]{:S(2)}, u32[]{:S(2)}) async-start(bf16[32,2,16384]{2,1,0:T(2,128)(2,1)} %reshape.43), calls=%async_computation.2 | async-start | bytes 4194304 | tf_op jit(solution)/shard_map/all_to_all | solution.py:55
Sparse Core Ops, SparseCore 0:
  11.6 71.4 all-gather.6
  86.8 78.7 all-gather.8
  169.2 79.4 all-gather.10
